TPU v7x, 32 devices: a whole 2x2x4 slice. The times are simulated.
32 devices in a mesh: dp: 8 (over z, core), mp: 4 (over y, x).
Axes of the slice: x: 2, y: 2, z: 4, core: 2. Of those that a mesh axis runs over, the one named last changes fastest.
Arguments:
- features: bfloat16 [8192, 8192], P('dp', 'mp'), may hold values from -6 to 6
- v_weight: bfloat16 [3, 8192, 1024], P(None, 'mp', 'dp'), may hold values from -0.0625 to 0.0625
- u_weight: bfloat16 [3, 1024, 8192], P(None, 'dp', 'mp'), may hold values from -0.1875 to 0.1875
- cross_bias: float32 [3, 8192], P(None, 'mp'), may hold values from -3 to 3
Outputs:
- crossed: bfloat16 [8192, 8192], P('dp', 'mp')
All inputs are finite; a program needn't handle non-finite values.
Results may differ from a plain program's by a relative error of at most 0.009.
Values may be sent and summed in bfloat16 or wider, within the bound.
A program may use at most 128 MiB of HBM per device.

v0:
```python
import functools

import jax
import jax.numpy as jnp
from jax import lax
from jax.experimental import pallas as pl
from jax.experimental.pallas import tpu as pltpu
from jax.sharding import PartitionSpec as P

MESH = pl.DeviceIdType.MESH
HOPS = (1, -1)


def kernel(nz, n, native, v_ref, u_ref, x_ref, b_ref, y_ref, wv, wu, f_ref, out_ref, pf, sbuf, rbuf,
           rank, loc, zsend, zrecv, fsend, psend, precv, rs_s, rs_r, ag_s, ag_r, in_s, out_s):
    layers, rs, cols = u_ref.shape
    rows = x_ref.shape[0]
    seg = rows // n
    ck = 2 * rs
    cb = 256 if cols % 256 == 0 else cols
    dp, me = lax.axis_index("dp"), lax.axis_index("mp")
    z, c = dp // 2, dp % 2
    step = jnp.where(2 * z < nz, 1, -1)

    def dev(zt, ct, m):
        return {"dp": zt * 2 + ct, "mp": m}

    def copy_to(src, dst, send, recv, device):
        return pltpu.make_async_remote_copy(
            src_ref=src, dst_ref=dst, send_sem=send, recv_sem=recv,
            device_id=device, device_id_type=MESH)

    def order(i):
        near = jnp.minimum(z, nz - 1 - z)
        zigzag = jnp.where(i % 2 == 1, -((i + 1) // 2), i // 2)
        return z + step * jnp.where(i <= 2 * near, zigzag, i - near)

    def valid(d):
        return (z + d >= 0) & (z + d < nz)

    def blk(p, s, cc):
        if native and p % 2 == 0:
            return wv.at[p // 2, s, :, pl.ds(pl.multiple_of(cc * rs, rs), rs)]
        w = wu if p % 2 else wv
        return w.at[p // 2, pl.ds(pl.multiple_of((s * 2 + cc) * rs, rs), rs)]

    def local_copy(p):
        src = (v_ref if p % 2 == 0 else u_ref).at[p // 2]
        return pltpu.make_async_copy(src, blk(p, z, c), loc.at[p])

    def direct(p, k):
        return copy_to(blk(p, z, c), blk(p, z, c), zsend.at[p, k], zrecv.at[p, z],
                       dev(z + HOPS[k], c, me))

    def arrival(p, s):
        return copy_to(blk(p, s, c), blk(p, s, c), fsend.at[p, s], zrecv.at[p, s], dev(z, 1 - c, me))

    def relays(s):
        return ((s > z) & (z >= 1)) | ((s < z) & (z <= nz - 2))

    def relay(p, s):
        return copy_to(blk(p, s, c), blk(p, s, c), fsend.at[p, s], zrecv.at[p, s],
                       dev(jnp.where(s > z, z - 1, z + 1), c, me))

    def push(p, s):
        return copy_to(blk(p, s, c), blk(p, s, c), psend.at[p, s], precv.at[p, s], dev(z, 1 - c, me))

    def pushed(p, s):
        return copy_to(blk(p, s, 1 - c), blk(p, s, 1 - c), psend.at[p, s], precv.at[p, s],
                       dev(z, 1 - c, me))

    def held(d):
        return (z >= 1) & (z <= nz - 2)

    def issue_own(p, first):
        for k in range(len(HOPS)):
            hold = held(HOPS[k])

            @pl.when(valid(HOPS[k]) & (jnp.logical_not(hold) if first else hold))
            def _():
                direct(p, k).start()

    def take(p, s):
        @pl.when(s != z)
        def _():
            arrival(p, s).wait_recv()

        @pl.when(relays(s))
        def _():
            relay(p, s).start()

        push(p, s).start()

    def lanes(s):
        return pl.ds(pl.multiple_of(s * ck, ck), ck)

    def seg_rows(m):
        return pl.ds(pl.multiple_of(m * seg, seg), seg)

    def other(k):
        return lax.rem(me + k, n)

    def block_out(j):
        at = pl.ds(pl.multiple_of(j * cb, cb), cb)
        return pltpu.make_async_copy(out_ref.at[:, at], y_ref.at[:, at], out_s.at[j])

    whole_in = pltpu.make_async_copy(x_ref, f_ref, in_s)
    for p in range(2 * layers):
        local_copy(p).start()
    whole_in.start()
    barrier = pltpu.get_barrier_semaphore()
    for k in range(1, n):
        pl.semaphore_signal(barrier, inc=1, device_id=dev(z, c, other(k)), device_id_type=MESH)
    pl.semaphore_signal(barrier, inc=1, device_id=dev(z, 1 - c, me), device_id_type=MESH)
    for d in HOPS:
        @pl.when(valid(d))
        def _():
            pl.semaphore_signal(barrier, inc=1, device_id=dev(z + d, c, me), device_id_type=MESH)
    pl.semaphore_wait(barrier, n + jnp.minimum(z, 1) + jnp.minimum(nz - 1 - z, 1))

    for p in range(2 * layers):
        local_copy(p).wait()
        issue_own(p, True)
        if p < 2:
            issue_own(p, False)
    whole_in.wait()

    for l in range(layers):
        pv, pu = 2 * l, 2 * l + 1
        cur = f_ref if l == 0 else out_ref

        def sum_out(s, k):
            t = other(k)
            return copy_to(sbuf.at[seg_rows(t), lanes(s)], rbuf.at[l, me, :, lanes(s)],
                           rs_s.at[s, k - 1], rs_r.at[s, me], dev(z, c, t))

        def sum_in(s, k):
            q = other(k)
            return copy_to(sbuf.at[seg_rows(q), lanes(s)], rbuf.at[l, q, :, lanes(s)],
                           rs_s.at[s, k - 1], rs_r.at[s, q], dev(z, c, q))

        def rank_out(s, k):
            mine = rank.at[l, seg_rows(me), lanes(s)]
            return copy_to(mine, mine, ag_s.at[s, k - 1], ag_r.at[s, me], dev(z, c, other(k)))

        def rank_in(s, k):
            q = other(k)
            theirs = rank.at[l, seg_rows(q), lanes(s)]
            return copy_to(theirs, theirs, ag_s.at[s, k - 1], ag_r.at[s, q], dev(z, c, q))

        def reduce(s):
            acc = pf[seg_rows(me), lanes(s)]
            for k in range(1, n):
                sum_in(s, k).wait_recv()
                acc = acc + rbuf[l, other(k), :, lanes(s)].astype(jnp.float32)
            rank[l, seg_rows(me), lanes(s)] = acc.astype(jnp.bfloat16)
            for k in range(1, n):
                rank_out(s, k).start()

        @pl.loop(0, nz)
        def _(i):
            s = order(i)
            take(pv, s)
            pushed(pv, s).wait_recv()
            if native:
                part = jnp.dot(cur[...], wv[l, s], preferred_element_type=jnp.float32)
            else:
                part = lax.dot_general(cur[...], wv[l, lanes(s), :], (((1,), (1,)), ((), ())),
                                       preferred_element_type=jnp.float32)
            pf[:, lanes(s)] = part
            sbuf[:, lanes(s)] = part.astype(jnp.bfloat16)
            for k in range(1, n):
                sum_out(s, k).start()

            @pl.when(i > 0)
            def _():
                reduce(order(i - 1))

        if pv + 2 < 2 * layers:
            issue_own(pv + 2, False)
        reduce(order(nz - 1))

        @pl.loop(0, nz)
        def _(i):
            take(pu, order(i))

        if pu + 2 < 2 * layers:
            issue_own(pu + 2, False)

        @pl.loop(0, nz)
        def _(i):
            s = order(i)
            pushed(pu, s).wait_recv()
            for k in range(1, n):
                rank_in(s, k).wait_recv()


        @pl.loop(0, cols // cb)
        def _(j):
            at = pl.ds(pl.multiple_of(j * cb, cb), cb)
            cross = jnp.dot(rank[l], wu[l, :, at], preferred_element_type=jnp.float32)
            cross = cross + b_ref[l, at][None, :]
            out_ref[:, at] = (f_ref[:, at].astype(jnp.float32) * cross
                              + cur[:, at].astype(jnp.float32)).astype(jnp.bfloat16)
            if l == layers - 1:
                @pl.when(j > 0)
                def _():
                    block_out(j - 1).start()

        if l == layers - 1:
            block_out(cols // cb - 1).start()

        @pl.loop(0, nz)
        def _(s):
            for k in range(1, n):
                sum_out(s, k).wait_send()
                rank_out(s, k).wait_send()

    for p in range(2 * layers):
        for k in range(len(HOPS)):
            @pl.when(valid(HOPS[k]))
            def _():
                direct(p, k).wait_send()

        @pl.loop(0, nz)
        def _(s):
            push(p, s).wait_send()

            @pl.when(relays(s))
            def _():
                relay(p, s).wait_send()

    @pl.loop(0, cols // cb)
    def _(j):
        block_out(j).wait()


def solution(mesh):
    n = mesh.shape["mp"]
    nz = mesh.shape["dp"] // 2

    def local(features, v_weight, u_weight, cross_bias):
        layers, rs, cols = u_weight.shape
        rows = features.shape[0]
        r = rs * nz * 2
        pieces = 2 * layers
        native = rs % 128 == 0
        v = v_weight if native else jnp.swapaxes(v_weight, 1, 2)
        vm = pl.BlockSpec(memory_space=pltpu.VMEM)
        hbm = pl.BlockSpec(memory_space=pl.ANY)
        dma = pltpu.SemaphoreType.DMA
        return pl.pallas_call(
            functools.partial(kernel, nz, n, native),
            out_shape=jax.ShapeDtypeStruct((rows, cols), jnp.bfloat16),
            in_specs=[hbm, hbm, hbm, vm],
            out_specs=hbm,
            scratch_shapes=[
                pltpu.VMEM((layers, nz, cols, 2 * rs) if native else (layers, r, cols), jnp.bfloat16),
                pltpu.VMEM((layers, r, cols), jnp.bfloat16),
                pltpu.VMEM((rows, cols), jnp.bfloat16),
                pltpu.VMEM((rows, cols), jnp.bfloat16),
                pltpu.VMEM((rows, r), jnp.float32),
                pltpu.VMEM((rows, r), jnp.bfloat16),
                pltpu.VMEM((layers, n, rows // n, r), jnp.bfloat16),
                pltpu.VMEM((layers, rows, r), jnp.bfloat16),
                dma((pieces,)), dma((pieces, len(HOPS))), dma((pieces, nz)), dma((pieces, nz)),
                dma((pieces, nz)), dma((pieces, nz)),
                dma((nz, n)), dma((nz, n)), dma((nz, n)), dma((nz, n)),
                dma, dma((cols // (256 if cols % 256 == 0 else cols),)),
            ],
            compiler_params=pltpu.CompilerParams(
                collective_id=0, has_side_effects=True, vmem_limit_bytes=67043328),
            name="cross_layers",
        )(v, u_weight, features, cross_bias)

    return jax.shard_map(
        local,
        mesh=mesh,
        in_specs=(P("dp", "mp"), P(None, "mp", "dp"), P(None, "dp", "mp"), P(None, "mp")),
        out_specs=P("dp", "mp"),
        check_vma=False,
    )
```

profile of v0, /device:TPU:0, one launch (start us, length us, event | category | flops | bytes accessed | tf_op | source)
XLA Modules:
  0.0 225.1 jit_solution(3810459461649968985)
XLA Ops:
  0.0 220.3 %cross_layers.1 = bf16[1024,2048]{1,0:T(8,128)(2,1)} custom-call(bf16[3,2048,128]{2,1,0:T(8,128)(2,1)} %v_ref.1, bf16[3,128,2048]{2,1,0:T(8,128)(2,1)} %u_ref.1, bf16[1024,2048]{1,0:T(8,128)(2,1)} %x_ref.1, f32[3,2048]{1,0:T(4,128)} %b_ref.1), custom_call_target="tpu_custom_call" | custom-call | tf_op jit(solution)/shard_map/cross_layers/pallas_call | solution.py:252
  220.3 4.8 %copy.6 = bf16[1024,2048]{1,0:T(8,128)(2,1)} copy(bf16[1024,2048]{1,0:T(8,128)(2,1)} %cross_layers.1) | data formatting | bytes 8388608
where the time goes:
time: 225 us
  Pallas kernels  220 us (98%)
  local copies, waits for them, and re-layouts  4.79 us (2%)
    pallas_call x1, Pallas kernels, local(): pl.pallas_call(functools.partial(kernel, nz, n, native), out_shape=jax.Sh...  220 us
    unnamed x1, local copies, waits for them, and re-layouts  4.79 us

commit v1 on v0

--- a/solution.py
+++ b/solution.py
@@ -11,16 +11,34 @@
 HOPS = (1, -1)
 
 
-def kernel(nz, n, native, v_ref, u_ref, x_ref, b_ref, y_ref, wv, wu, f_ref, out_ref, pf, sbuf, rbuf,
-           rank, loc, zsend, zrecv, fsend, psend, precv, rs_s, rs_r, ag_s, ag_r, in_s, out_s):
+def kernel(nz, n, native, nb, v_ref, u_ref, x_ref, b_ref, out_ref, wv, wu, f_ref, pf, sbuf, rbuf,
+           rank, loc, zsend, zrecv, fsend, psend, precv, rs_s, rs_r, ag_s, ag_r, in_s):
     layers, rs, cols = u_ref.shape
     rows = x_ref.shape[0]
     seg = rows // n
     ck = 2 * rs
+    tail = 2 * layers - 1
+    pieces = tail + nb
+    bw = cols // nb
+
+    def at_sem(p):
+        return tail + p[0] if isinstance(p, tuple) else p
+
+    def each_piece(body):
+        for p in range(tail):
+            body(p)
+        each_tail(body)
+
+    def each_tail(body):
+        @pl.loop(0, nb)
+        def _(b):
+            body((b,))
+
     cb = 256 if cols % 256 == 0 else cols
     dp, me = lax.axis_index("dp"), lax.axis_index("mp")
     z, c = dp // 2, dp % 2
     step = jnp.where(2 * z < nz, 1, -1)
+    end = (z == 0) | (z == nz - 1)
 
     def dev(zt, ct, m):
         return {"dp": zt * 2 + ct, "mp": m}
@@ -39,34 +57,40 @@
         return (z + d >= 0) & (z + d < nz)
 
     def blk(p, s, cc):
+        if isinstance(p, tuple):
+            return wu.at[layers - 1, pl.ds(pl.multiple_of((s * 2 + cc) * rs, rs), rs),
+                         pl.ds(pl.multiple_of(p[0] * bw, bw), bw)]
         if native and p % 2 == 0:
             return wv.at[p // 2, s, :, pl.ds(pl.multiple_of(cc * rs, rs), rs)]
         w = wu if p % 2 else wv
         return w.at[p // 2, pl.ds(pl.multiple_of((s * 2 + cc) * rs, rs), rs)]
 
     def local_copy(p):
-        src = (v_ref if p % 2 == 0 else u_ref).at[p // 2]
-        return pltpu.make_async_copy(src, blk(p, z, c), loc.at[p])
+        if isinstance(p, tuple):
+            src = u_ref.at[layers - 1, :, pl.ds(pl.multiple_of(p[0] * bw, bw), bw)]
+        else:
+            src = (v_ref if p % 2 == 0 else u_ref).at[p // 2]
+        return pltpu.make_async_copy(src, blk(p, z, c), loc.at[at_sem(p)])
 
     def direct(p, k):
-        return copy_to(blk(p, z, c), blk(p, z, c), zsend.at[p, k], zrecv.at[p, z],
+        return copy_to(blk(p, z, c), blk(p, z, c), zsend.at[at_sem(p), k], zrecv.at[at_sem(p), z],
                        dev(z + HOPS[k], c, me))
 
     def arrival(p, s):
-        return copy_to(blk(p, s, c), blk(p, s, c), fsend.at[p, s], zrecv.at[p, s], dev(z, 1 - c, me))
+        return copy_to(blk(p, s, c), blk(p, s, c), fsend.at[at_sem(p), s], zrecv.at[at_sem(p), s], dev(z, 1 - c, me))
 
     def relays(s):
         return ((s > z) & (z >= 1)) | ((s < z) & (z <= nz - 2))
 
     def relay(p, s):
-        return copy_to(blk(p, s, c), blk(p, s, c), fsend.at[p, s], zrecv.at[p, s],
+        return copy_to(blk(p, s, c), blk(p, s, c), fsend.at[at_sem(p), s], zrecv.at[at_sem(p), s],
                        dev(jnp.where(s > z, z - 1, z + 1), c, me))
 
     def push(p, s):
-        return copy_to(blk(p, s, c), blk(p, s, c), psend.at[p, s], precv.at[p, s], dev(z, 1 - c, me))
+        return copy_to(blk(p, s, c), blk(p, s, c), psend.at[at_sem(p), s], precv.at[at_sem(p), s], dev(z, 1 - c, me))
 
     def pushed(p, s):
-        return copy_to(blk(p, s, 1 - c), blk(p, s, 1 - c), psend.at[p, s], precv.at[p, s],
+        return copy_to(blk(p, s, 1 - c), blk(p, s, 1 - c), psend.at[at_sem(p), s], precv.at[at_sem(p), s],
                        dev(z, 1 - c, me))
 
     def held(d):
@@ -100,13 +124,22 @@
     def other(k):
         return lax.rem(me + k, n)
 
-    def block_out(j):
-        at = pl.ds(pl.multiple_of(j * cb, cb), cb)
-        return pltpu.make_async_copy(out_ref.at[:, at], y_ref.at[:, at], out_s.at[j])
+    def drain(p):
+        for k in range(len(HOPS)):
+            @pl.when(valid(HOPS[k]))
+            def _():
+                direct(p, k).wait_send()
+
+        @pl.loop(0, nz)
+        def _(s):
+            push(p, s).wait_send()
+
+            @pl.when(relays(s))
+            def _():
+                relay(p, s).wait_send()
 
     whole_in = pltpu.make_async_copy(x_ref, f_ref, in_s)
-    for p in range(2 * layers):
-        local_copy(p).start()
+    each_piece(lambda p: local_copy(p).start())
     whole_in.start()
     barrier = pltpu.get_barrier_semaphore()
     for k in range(1, n):
@@ -118,12 +151,25 @@
             pl.semaphore_signal(barrier, inc=1, device_id=dev(z + d, c, me), device_id_type=MESH)
     pl.semaphore_wait(barrier, n + jnp.minimum(z, 1) + jnp.minimum(nz - 1 - z, 1))
 
-    for p in range(2 * layers):
+    def first_sends(p):
         local_copy(p).wait()
         issue_own(p, True)
-        if p < 2:
+        if p in range(min(2, tail)):
             issue_own(p, False)
+
+    each_piece(first_sends)
     whole_in.wait()
+
+    @pl.when(jnp.logical_not(end))
+    def _():
+        @pl.loop(0, nz)
+        def _(i):
+            take(0, order(i))
+
+    if layers > 1:
+        issue_own(2, False)
+    else:
+        each_tail(lambda p: issue_own(p, False))
 
     for l in range(layers):
         pv, pu = 2 * l, 2 * l + 1
@@ -157,10 +203,21 @@
             for k in range(1, n):
                 rank_out(s, k).start()
 
+        last = l == layers - 1
+        each_up = each_tail if last else lambda body: body(pu)
+
         @pl.loop(0, nz)
         def _(i):
             s = order(i)
-            take(pv, s)
+
+            @pl.when(end)
+            def _():
+                take(pv, s)
+
+            @pl.when(jnp.logical_not(end))
+            def _():
+                each_up(lambda p: take(p, s))
+
             pushed(pv, s).wait_recv()
             if native:
                 part = jnp.dot(cur[...], wv[l, s], preferred_element_type=jnp.float32)
@@ -176,39 +233,64 @@
             def _():
                 reduce(order(i - 1))
 
-        if pv + 2 < 2 * layers:
+        if pu + 2 < tail:
+            issue_own(pu + 2, False)
+        elif not last and layers > 2:
             issue_own(pv + 2, False)
+
         reduce(order(nz - 1))
-
-        @pl.loop(0, nz)
-        def _(i):
-            take(pu, order(i))
-
-        if pu + 2 < 2 * layers:
-            issue_own(pu + 2, False)
-
-        @pl.loop(0, nz)
+        if last:
+            for p in range(tail - 1):
+                drain(p)
+
+        @pl.loop(0, nz - 1)
         def _(i):
             s = order(i)
-            pushed(pu, s).wait_recv()
-            for k in range(1, n):
-                rank_in(s, k).wait_recv()
-
-
-        @pl.loop(0, cols // cb)
-        def _(j):
-            at = pl.ds(pl.multiple_of(j * cb, cb), cb)
-            cross = jnp.dot(rank[l], wu[l, :, at], preferred_element_type=jnp.float32)
-            cross = cross + b_ref[l, at][None, :]
-            out_ref[:, at] = (f_ref[:, at].astype(jnp.float32) * cross
-                              + cur[:, at].astype(jnp.float32)).astype(jnp.bfloat16)
-            if l == layers - 1:
-                @pl.when(j > 0)
+
+            @pl.when(end)
+            def _():
+                each_up(lambda p: take(p, s))
+
+            if not last:
+                @pl.when(jnp.logical_not(end))
                 def _():
-                    block_out(j - 1).start()
-
-        if l == layers - 1:
-            block_out(cols // cb - 1).start()
+                    take(pv + 2, s)
+
+        if not last:
+            @pl.when(jnp.logical_not(end))
+            def _():
+                take(pv + 2, order(nz - 1))
+
+            if pv + 4 < tail - 1:
+                issue_own(pv + 4, False)
+            elif pv + 4 > tail:
+                each_tail(lambda p: issue_own(p, False))
+
+        @pl.loop(0, nz)
+        def _(i):
+            for k in range(1, n):
+                rank_in(order(i), k).wait_recv()
+
+        def finish(p):
+            @pl.when(end)
+            def _():
+                take(p, order(nz - 1))
+
+            @pl.loop(0, nz)
+            def _(i):
+                pushed(p, order(i)).wait_recv()
+
+            width, base = (bw, p[0] * bw) if last else (cols, 0)
+
+            @pl.loop(0, width // cb)
+            def _(j):
+                at = pl.ds(pl.multiple_of(base + j * cb, cb), cb)
+                cross = jnp.dot(rank[l], wu[l, :, at], preferred_element_type=jnp.float32)
+                cross = cross + b_ref[l, at][None, :]
+                out_ref[:, at] = (f_ref[:, at].astype(jnp.float32) * cross
+                                  + cur[:, at].astype(jnp.float32)).astype(jnp.bfloat16)
+
+        each_up(finish)
 
         @pl.loop(0, nz)
         def _(s):
@@ -216,23 +298,9 @@
                 sum_out(s, k).wait_send()
                 rank_out(s, k).wait_send()
 
-    for p in range(2 * layers):
-        for k in range(len(HOPS)):
-            @pl.when(valid(HOPS[k]))
-            def _():
-                direct(p, k).wait_send()
-
-        @pl.loop(0, nz)
-        def _(s):
-            push(p, s).wait_send()
-
-            @pl.when(relays(s))
-            def _():
-                relay(p, s).wait_send()
-
-    @pl.loop(0, cols // cb)
-    def _(j):
-        block_out(j).wait()
+    for p in range(max(tail - 1, 0), tail):
+        drain(p)
+    each_tail(drain)
 
 
 def solution(mesh):
@@ -243,21 +311,21 @@
         layers, rs, cols = u_weight.shape
         rows = features.shape[0]
         r = rs * nz * 2
-        pieces = 2 * layers
+        nb = 4 if cols % 512 == 0 else 1
+        pieces = 2 * layers - 1 + nb
         native = rs % 128 == 0
         v = v_weight if native else jnp.swapaxes(v_weight, 1, 2)
         vm = pl.BlockSpec(memory_space=pltpu.VMEM)
         hbm = pl.BlockSpec(memory_space=pl.ANY)
         dma = pltpu.SemaphoreType.DMA
         return pl.pallas_call(
-            functools.partial(kernel, nz, n, native),
-            out_shape=jax.ShapeDtypeStruct((rows, cols), jnp.bfloat16),
+            functools.partial(kernel, nz, n, native, nb),
+            out_shape=pltpu.VMEM((rows, cols), jnp.bfloat16),
             in_specs=[hbm, hbm, hbm, vm],
-            out_specs=hbm,
+            out_specs=vm,
             scratch_shapes=[
                 pltpu.VMEM((layers, nz, cols, 2 * rs) if native else (layers, r, cols), jnp.bfloat16),
                 pltpu.VMEM((layers, r, cols), jnp.bfloat16),
-                pltpu.VMEM((rows, cols), jnp.bfloat16),
                 pltpu.VMEM((rows, cols), jnp.bfloat16),
                 pltpu.VMEM((rows, r), jnp.float32),
                 pltpu.VMEM((rows, r), jnp.bfloat16),
@@ -266,10 +334,10 @@
                 dma((pieces,)), dma((pieces, len(HOPS))), dma((pieces, nz)), dma((pieces, nz)),
                 dma((pieces, nz)), dma((pieces, nz)),
                 dma((nz, n)), dma((nz, n)), dma((nz, n)), dma((nz, n)),
-                dma, dma((cols // (256 if cols % 256 == 0 else cols),)),
+                dma,
             ],
             compiler_params=pltpu.CompilerParams(
-                collective_id=0, has_side_effects=True, vmem_limit_bytes=67043328),
+                collective_id=0, has_side_effects=True, vmem_limit_bytes=59*2**20),
             name="cross_layers",
         )(v, u_weight, features, cross_bias)
 

time: 225 us -> 219 us (0.973)
  Pallas kernels: 220 us -> 217 us
  local copies, waits for them, and re-layouts: 4.79 us -> 2.02 us
    pallas_call x1, Pallas kernels: 220 us -> 217 us  [local(): pl.pallas_call(functools.partial(kernel, nz, n, native, nb), out_shape=pl...]
    unnamed x1, local copies, waits for them, and re-layouts: 4.79 us -> 2.02 us
where the time goes in v1:
time: 219 us
  Pallas kernels  217 us (99%)
    pallas_call x1, Pallas kernels, local(): pl.pallas_call(functools.partial(kernel, nz, n, native, nb), out_shape=pl...  217 us

profile of v1, /device:TPU:0, one launch (start us, length us, event | category | flops | bytes accessed | tf_op | source)
XLA Modules:
  0.0 218.6 jit_solution(2324866083217303919)
XLA Ops:
  0.0 216.5 %cross_layers.1 = bf16[1024,2048]{1,0:T(8,128)(2,1)S(1)} custom-call(bf16[3,2048,128]{2,1,0:T(8,128)(2,1)} %v_ref.1, bf16[3,128,2048]{2,1,0:T(8,128)(2,1)} %u_ref.1, bf16[1024,2048]{1,0:T(8,128)(2,1)} %x_ref.1, f32[3,2048]{1,0:T(4,128)} %b_ref.1), custom_call_target="tpu_custom_call" | custom-call | tf_op jit(solution)/shard_map/cross_layers/pallas_call | solution.py:321
  216.6 2.0 copy.6

commit v2 on v1

--- a/solution.py
+++ b/solution.py
@@ -96,11 +96,14 @@
     def held(d):
         return (z >= 1) & (z <= nz - 2)
 
-    def issue_own(p, first):
+    def to_end(k):
+        return (z + HOPS[k] == 0) | (z + HOPS[k] == nz - 1)
+
+    def issue_own(p, first, k_ok=lambda k: True):
         for k in range(len(HOPS)):
             hold = held(HOPS[k])
 
-            @pl.when(valid(HOPS[k]) & (jnp.logical_not(hold) if first else hold))
+            @pl.when(valid(HOPS[k]) & (jnp.logical_not(hold) if first else hold) & (k_ok(k)))
             def _():
                 direct(p, k).start()
 
@@ -124,14 +127,15 @@
     def other(k):
         return lax.rem(me + k, n)
 
-    def drain(p):
+    def drain(p, pushes=nz):
         for k in range(len(HOPS)):
             @pl.when(valid(HOPS[k]))
             def _():
                 direct(p, k).wait_send()
 
-        @pl.loop(0, nz)
-        def _(s):
+        @pl.loop(0, pushes)
+        def _(i):
+            s = order(i)
             push(p, s).wait_send()
 
             @pl.when(relays(s))
@@ -139,8 +143,6 @@
                 relay(p, s).wait_send()
 
     whole_in = pltpu.make_async_copy(x_ref, f_ref, in_s)
-    each_piece(lambda p: local_copy(p).start())
-    whole_in.start()
     barrier = pltpu.get_barrier_semaphore()
     for k in range(1, n):
         pl.semaphore_signal(barrier, inc=1, device_id=dev(z, c, other(k)), device_id_type=MESH)
@@ -149,13 +151,17 @@
         @pl.when(valid(d))
         def _():
             pl.semaphore_signal(barrier, inc=1, device_id=dev(z + d, c, me), device_id_type=MESH)
+    each_piece(lambda p: local_copy(p).start())
+    whole_in.start()
     pl.semaphore_wait(barrier, n + jnp.minimum(z, 1) + jnp.minimum(nz - 1 - z, 1))
 
     def first_sends(p):
         local_copy(p).wait()
         issue_own(p, True)
-        if p in range(min(2, tail)):
+        if p == 0:
             issue_own(p, False)
+        if p == 1:
+            issue_own(p, False, to_end)
 
     each_piece(first_sends)
     whole_in.wait()
@@ -166,6 +172,8 @@
         def _(i):
             take(0, order(i))
 
+    if tail > 1:
+        issue_own(1, False, lambda k: jnp.logical_not(to_end(k)))
     if layers > 1:
         issue_own(2, False)
     else:
@@ -209,6 +217,10 @@
         @pl.loop(0, nz)
         def _(i):
             s = order(i)
+
+            @pl.when(i == nz - 1)
+            def _():
+                reduce(order(i - 1))
 
             @pl.when(end)
             def _():
@@ -229,7 +241,7 @@
             for k in range(1, n):
                 sum_out(s, k).start()
 
-            @pl.when(i > 0)
+            @pl.when((i > 0) & (i < nz - 1))
             def _():
                 reduce(order(i - 1))
 
@@ -239,9 +251,6 @@
             issue_own(pv + 2, False)
 
         reduce(order(nz - 1))
-        if last:
-            for p in range(tail - 1):
-                drain(p)
 
         @pl.loop(0, nz - 1)
         def _(i):
@@ -266,15 +275,32 @@
             elif pv + 4 > tail:
                 each_tail(lambda p: issue_own(p, False))
 
+        if last:
+            @pl.when(end)
+            def _():
+                for p in range(tail):
+                    drain(p)
+                each_tail(lambda p: drain(p, nz - 1))
+
         @pl.loop(0, nz)
         def _(i):
             for k in range(1, n):
                 rank_in(order(i), k).wait_recv()
 
+        if last:
+            @pl.when(end)
+            def _():
+                take((0,), order(nz - 1))
+
         def finish(p):
             @pl.when(end)
             def _():
-                take(p, order(nz - 1))
+                if last:
+                    @pl.when(p[0] < nb - 1)
+                    def _():
+                        take((p[0] + 1,), order(nz - 1))
+                else:
+                    take(p, order(nz - 1))
 
             @pl.loop(0, nz)
             def _(i):
@@ -290,17 +316,23 @@
                 out_ref[:, at] = (f_ref[:, at].astype(jnp.float32) * cross
                                   + cur[:, at].astype(jnp.float32)).astype(jnp.bfloat16)
 
-        each_up(finish)
-
         @pl.loop(0, nz)
         def _(s):
             for k in range(1, n):
                 sum_out(s, k).wait_send()
                 rank_out(s, k).wait_send()
 
-    for p in range(max(tail - 1, 0), tail):
-        drain(p)
-    each_tail(drain)
+        each_up(finish)
+
+    @pl.when(end)
+    def _():
+        each_tail(lambda p: push(p, order(nz - 1)).wait_send())
+
+    @pl.when(jnp.logical_not(end))
+    def _():
+        for p in range(tail):
+            drain(p)
+        each_tail(drain)
 
 
 def solution(mesh):

time: 219 us -> 216 us (0.986)
  Pallas kernels: 217 us -> 214 us
    pallas_call x1, Pallas kernels: 217 us -> 214 us  [local(): pl.pallas_call(functools.partial(kernel, nz, n, native, nb), out_shape=pl...]
where the time goes in v2:
time: 216 us
  Pallas kernels  214 us (99%)
    pallas_call x1, Pallas kernels, local(): pl.pallas_call(functools.partial(kernel, nz, n, native, nb), out_shape=pl...  214 us

profile of v2, /device:TPU:0, one launch (start us, length us, event | category | flops | bytes accessed | tf_op | source)
XLA Modules:
  0.0 216.1 jit_solution(2026758989288551480)
XLA Ops:
  0.0 214.1 %cross_layers.1 = bf16[1024,2048]{1,0:T(8,128)(2,1)S(1)} custom-call(bf16[3,2048,128]{2,1,0:T(8,128)(2,1)} %v_ref.1, bf16[3,128,2048]{2,1,0:T(8,128)(2,1)} %u_ref.1, bf16[1024,2048]{1,0:T(8,128)(2,1)} %x_ref.1, f32[3,2048]{1,0:T(4,128)} %b_ref.1), custom_call_target="tpu_custom_call" | custom-call | tf_op jit(solution)/shard_map/cross_layers/pallas_call | solution.py:353
  214.1 2.0 copy.6

commit v3 on v2

--- a/solution.py
+++ b/solution.py
@@ -12,7 +12,7 @@
 
 
 def kernel(nz, n, native, nb, v_ref, u_ref, x_ref, b_ref, out_ref, wv, wu, f_ref, pf, sbuf, rbuf,
-           rank, loc, zsend, zrecv, fsend, psend, precv, rs_s, rs_r, ag_s, ag_r, in_s):
+           rank, loc, zsend, zrecv, fsend, psend, vrecv, urecv, rs_s, rs_r, ag_s, ag_r, in_s):
     layers, rs, cols = u_ref.shape
     rows = x_ref.shape[0]
     seg = rows // n
@@ -23,6 +23,9 @@
 
     def at_sem(p):
         return tail + p[0] if isinstance(p, tuple) else p
+
+    def factor(p):
+        return tail if isinstance(p, tuple) else p
 
     def each_piece(body):
         for p in range(tail):
@@ -70,28 +73,46 @@
             src = u_ref.at[layers - 1, :, pl.ds(pl.multiple_of(p[0] * bw, bw), bw)]
         else:
             src = (v_ref if p % 2 == 0 else u_ref).at[p // 2]
-        return pltpu.make_async_copy(src, blk(p, z, c), loc.at[at_sem(p)])
+        return pltpu.make_async_copy(src, blk(p, z, c), loc)
 
     def direct(p, k):
-        return copy_to(blk(p, z, c), blk(p, z, c), zsend.at[at_sem(p), k], zrecv.at[at_sem(p), z],
-                       dev(z + HOPS[k], c, me))
+        return copy_to(blk(p, z, c), blk(p, z, c), zsend.at[factor(p)],
+                       zrecv.at[at_sem(p), z], dev(z + HOPS[k], c, me))
 
     def arrival(p, s):
-        return copy_to(blk(p, s, c), blk(p, s, c), fsend.at[at_sem(p), s], zrecv.at[at_sem(p), s], dev(z, 1 - c, me))
+        return copy_to(blk(p, s, c), blk(p, s, c), fsend.at[factor(p)],
+                       zrecv.at[at_sem(p), s], dev(z, 1 - c, me))
 
     def relays(s):
         return ((s > z) & (z >= 1)) | ((s < z) & (z <= nz - 2))
 
     def relay(p, s):
-        return copy_to(blk(p, s, c), blk(p, s, c), fsend.at[at_sem(p), s], zrecv.at[at_sem(p), s],
+        return copy_to(blk(p, s, c), blk(p, s, c), fsend.at[factor(p)], zrecv.at[at_sem(p), s],
                        dev(jnp.where(s > z, z - 1, z + 1), c, me))
 
+    def landed(p, s):
+        if isinstance(p, tuple):
+            return urecv.at[layers - 1 + p[0]]
+        return urecv.at[p // 2] if p % 2 else vrecv.at[p // 2, s]
+
     def push(p, s):
-        return copy_to(blk(p, s, c), blk(p, s, c), psend.at[at_sem(p), s], precv.at[at_sem(p), s], dev(z, 1 - c, me))
-
-    def pushed(p, s):
-        return copy_to(blk(p, s, 1 - c), blk(p, s, 1 - c), psend.at[at_sem(p), s], precv.at[at_sem(p), s],
-                       dev(z, 1 - c, me))
+        return copy_to(blk(p, s, c), blk(p, s, c), psend.at[factor(p)], landed(p, s), dev(z, 1 - c, me))
+
+    def halves(p, count):
+        if isinstance(p, tuple):
+            return wu.at[layers - 1, pl.ds(0, count * rs),
+                         pl.ds(pl.multiple_of(p[0] * bw, bw), bw)]
+        if native and p % 2 == 0:
+            return wv.at[p // 2, pl.ds(0, count), :, pl.ds(0, rs)]
+        return (wu if p % 2 else wv).at[p // 2, pl.ds(0, count * rs)]
+
+    def pushed(p, s=None):
+        ref = halves(p, nz) if s is None else blk(p, s, 1 - c)
+        return copy_to(ref, ref, psend.at[factor(p)], landed(p, s), dev(z, 1 - c, me))
+
+    def sent(sem, p, count):
+        ref = halves(p, count)
+        copy_to(ref, ref, sem.at[p], vrecv.at[0, 0], dev(z, 1 - c, me)).wait_send()
 
     def held(d):
         return (z >= 1) & (z <= nz - 2)
@@ -126,21 +147,6 @@
 
     def other(k):
         return lax.rem(me + k, n)
-
-    def drain(p, pushes=nz):
-        for k in range(len(HOPS)):
-            @pl.when(valid(HOPS[k]))
-            def _():
-                direct(p, k).wait_send()
-
-        @pl.loop(0, pushes)
-        def _(i):
-            s = order(i)
-            push(p, s).wait_send()
-
-            @pl.when(relays(s))
-            def _():
-                relay(p, s).wait_send()
 
     whole_in = pltpu.make_async_copy(x_ref, f_ref, in_s)
     barrier = pltpu.get_barrier_semaphore()
@@ -156,13 +162,13 @@
     pl.semaphore_wait(barrier, n + jnp.minimum(z, 1) + jnp.minimum(nz - 1 - z, 1))
 
     def first_sends(p):
-        local_copy(p).wait()
         issue_own(p, True)
         if p == 0:
             issue_own(p, False)
         if p == 1:
             issue_own(p, False, to_end)
 
+    each_piece(lambda p: local_copy(p).wait())
     each_piece(first_sends)
     whole_in.wait()
 
@@ -179,6 +185,9 @@
     else:
         each_tail(lambda p: issue_own(p, False))
 
+    def early(p):
+        return {0: 0, 2: min(2, nz)}.get(p, 1)
+
     for l in range(layers):
         pv, pu = 2 * l, 2 * l + 1
         cur = f_ref if l == 0 else out_ref
@@ -186,26 +195,25 @@
         def sum_out(s, k):
             t = other(k)
             return copy_to(sbuf.at[seg_rows(t), lanes(s)], rbuf.at[l, me, :, lanes(s)],
-                           rs_s.at[s, k - 1], rs_r.at[s, me], dev(z, c, t))
-
-        def sum_in(s, k):
-            q = other(k)
-            return copy_to(sbuf.at[seg_rows(q), lanes(s)], rbuf.at[l, q, :, lanes(s)],
-                           rs_s.at[s, k - 1], rs_r.at[s, q], dev(z, c, q))
+                           rs_s, rs_r.at[s], dev(z, c, t))
+
+        def sums_in(s):
+            ref = rbuf.at[l, pl.ds(0, n - 1), :, lanes(s)]
+            return copy_to(ref, ref, rs_s, rs_r.at[s], dev(z, 1 - c, me))
 
         def rank_out(s, k):
             mine = rank.at[l, seg_rows(me), lanes(s)]
-            return copy_to(mine, mine, ag_s.at[s, k - 1], ag_r.at[s, me], dev(z, c, other(k)))
-
-        def rank_in(s, k):
-            q = other(k)
-            theirs = rank.at[l, seg_rows(q), lanes(s)]
-            return copy_to(theirs, theirs, ag_s.at[s, k - 1], ag_r.at[s, q], dev(z, c, q))
+            return copy_to(mine, mine, ag_s, ag_r, dev(z, c, other(k)))
+
+        sums = sbuf.at[pl.ds(0, (n - 1) * seg)]
+        ranks = rank.at[l, pl.ds(0, (n - 1) * seg)]
+        sums_all = copy_to(sums, sums, rs_s, ag_r, dev(z, 1 - c, me))
+        ranks_all = copy_to(ranks, ranks, ag_s, ag_r, dev(z, 1 - c, me))
 
         def reduce(s):
             acc = pf[seg_rows(me), lanes(s)]
+            sums_in(s).wait_recv()
             for k in range(1, n):
-                sum_in(s, k).wait_recv()
                 acc = acc + rbuf[l, other(k), :, lanes(s)].astype(jnp.float32)
             rank[l, seg_rows(me), lanes(s)] = acc.astype(jnp.bfloat16)
             for k in range(1, n):
@@ -222,7 +230,7 @@
             def _():
                 reduce(order(i - 1))
 
-            @pl.when(end)
+            @pl.when(end & (i >= early(pv)))
             def _():
                 take(pv, s)
 
@@ -279,13 +287,19 @@
             @pl.when(end)
             def _():
                 for p in range(tail):
-                    drain(p)
-                each_tail(lambda p: drain(p, nz - 1))
-
-        @pl.loop(0, nz)
-        def _(i):
-            for k in range(1, n):
-                rank_in(order(i), k).wait_recv()
+                    sent(zsend, p, 1)
+                    sent(psend, p, nz)
+                sent(zsend, tail, 1)
+
+        if not last:
+            @pl.when(end)
+            def _():
+                for i in range(early(pv + 2)):
+                    take(pv + 2, order(i))
+
+        ranks_all.wait_recv()
+        sums_all.wait_send()
+        ranks_all.wait_send()
 
         if last:
             @pl.when(end)
@@ -302,10 +316,7 @@
                 else:
                     take(p, order(nz - 1))
 
-            @pl.loop(0, nz)
-            def _(i):
-                pushed(p, order(i)).wait_recv()
-
+            pushed(p).wait_recv()
             width, base = (bw, p[0] * bw) if last else (cols, 0)
 
             @pl.loop(0, width // cb)
@@ -316,23 +327,17 @@
                 out_ref[:, at] = (f_ref[:, at].astype(jnp.float32) * cross
                                   + cur[:, at].astype(jnp.float32)).astype(jnp.bfloat16)
 
-        @pl.loop(0, nz)
-        def _(s):
-            for k in range(1, n):
-                sum_out(s, k).wait_send()
-                rank_out(s, k).wait_send()
-
         each_up(finish)
 
-    @pl.when(end)
-    def _():
-        each_tail(lambda p: push(p, order(nz - 1)).wait_send())
+    sent(psend, tail, nz)
 
     @pl.when(jnp.logical_not(end))
     def _():
-        for p in range(tail):
-            drain(p)
-        each_tail(drain)
+        for p in range(tail + 1):
+            sent(zsend, p, 2)
+            sent(fsend, p, nz - 1)
+            if p < tail:
+                sent(psend, p, nz)
 
 
 def solution(mesh):
@@ -343,7 +348,7 @@
         layers, rs, cols = u_weight.shape
         rows = features.shape[0]
         r = rs * nz * 2
-        nb = 4 if cols % 512 == 0 else 1
+        nb = 8 if cols % 2048 == 0 else 1
         pieces = 2 * layers - 1 + nb
         native = rs % 128 == 0
         v = v_weight if native else jnp.swapaxes(v_weight, 1, 2)
@@ -363,10 +368,9 @@
                 pltpu.VMEM((rows, r), jnp.bfloat16),
                 pltpu.VMEM((layers, n, rows // n, r), jnp.bfloat16),
                 pltpu.VMEM((layers, rows, r), jnp.bfloat16),
-                dma((pieces,)), dma((pieces, len(HOPS))), dma((pieces, nz)), dma((pieces, nz)),
-                dma((pieces, nz)), dma((pieces, nz)),
-                dma((nz, n)), dma((nz, n)), dma((nz, n)), dma((nz, n)),
-                dma,
+                dma, dma((2 * layers,)), dma((pieces, nz)), dma((2 * layers,)), dma((2 * layers,)),
+                dma((layers, nz)), dma((layers - 1 + nb,)),
+                dma, dma((nz,)), dma, dma, dma,
             ],
             compiler_params=pltpu.CompilerParams(
                 collective_id=0, has_side_effects=True, vmem_limit_bytes=59*2**20),

time: 216 us -> 214 us (level)
    pallas_call x1, Pallas kernels: 214 us -> 212 us  [local(): pl.pallas_call(functools.partial(kernel, nz, n, native, nb), out_shape=pl...]
where the time goes in v3:
time: 214 us
  Pallas kernels  212 us (99%)
    pallas_call x1, Pallas kernels, local(): pl.pallas_call(functools.partial(kernel, nz, n, native, nb), out_shape=pl...  212 us

profile of v3, /device:TPU:0, one launch (start us, length us, event | category | flops | bytes accessed | tf_op | source)
XLA Modules:
  0.0 213.7 jit_solution(17095702121263747804)
XLA Ops:
  0.0 211.7 %cross_layers.1 = bf16[1024,2048]{1,0:T(8,128)(2,1)S(1)} custom-call(bf16[3,2048,128]{2,1,0:T(8,128)(2,1)} %v_ref.1, bf16[3,128,2048]{2,1,0:T(8,128)(2,1)} %u_ref.1, bf16[1024,2048]{1,0:T(8,128)(2,1)} %x_ref.1, f32[3,2048]{1,0:T(4,128)} %b_ref.1), custom_call_target="tpu_custom_call" | custom-call | tf_op jit(solution)/shard_map/cross_layers/pallas_call | solution.py:358
  211.7 2.0 copy.6

commit v4 on v3

--- a/solution.py
+++ b/solution.py
@@ -9,10 +9,11 @@
 
 MESH = pl.DeviceIdType.MESH
 HOPS = (1, -1)
+TO_Y = (0, 1, 0, 1, 1, 0, 0, 1, 1, 0)
 
 
 def kernel(nz, n, native, nb, v_ref, u_ref, x_ref, b_ref, out_ref, wv, wu, f_ref, pf, sbuf, rbuf,
-           rank, loc, zsend, zrecv, fsend, psend, vrecv, urecv, rs_s, rs_r, ag_s, ag_r, in_s):
+           rank, loc, zsend, zrecv, fsend, psend, vrecv, urecv, cbuf, rs_s, cb_s, ag_s, rs_r, cb_r, ag_r, all_r, in_s):
     layers, rs, cols = u_ref.shape
     rows = x_ref.shape[0]
     seg = rows // n
@@ -26,11 +27,6 @@
 
     def factor(p):
         return tail if isinstance(p, tuple) else p
-
-    def each_piece(body):
-        for p in range(tail):
-            body(p)
-        each_tail(body)
 
     def each_tail(body):
         @pl.loop(0, nb)
@@ -73,7 +69,7 @@
             src = u_ref.at[layers - 1, :, pl.ds(pl.multiple_of(p[0] * bw, bw), bw)]
         else:
             src = (v_ref if p % 2 == 0 else u_ref).at[p // 2]
-        return pltpu.make_async_copy(src, blk(p, z, c), loc)
+        return pltpu.make_async_copy(src, blk(p, z, c), loc.at[0 if p == 0 else 1])
 
     def direct(p, k):
         return copy_to(blk(p, z, c), blk(p, z, c), zsend.at[factor(p)],
@@ -145,21 +141,26 @@
     def seg_rows(m):
         return pl.ds(pl.multiple_of(m * seg, seg), seg)
 
+    def half(m, h):
+        return pl.ds(pl.multiple_of(m * seg + h * (seg // 2), seg // 2), seg // 2)
+
+    two = n == 4
+    peers = (me + 1 - 2 * (me % 2), lax.rem(me + 2, n), n - 1 - me, me)
+
     def other(k):
         return lax.rem(me + k, n)
 
     whole_in = pltpu.make_async_copy(x_ref, f_ref, in_s)
     barrier = pltpu.get_barrier_semaphore()
-    for k in range(1, n):
-        pl.semaphore_signal(barrier, inc=1, device_id=dev(z, c, other(k)), device_id_type=MESH)
+    for m in peers[:2] if two else [other(k) for k in range(1, n)]:
+        pl.semaphore_signal(barrier, inc=1, device_id=dev(z, c, m), device_id_type=MESH)
     pl.semaphore_signal(barrier, inc=1, device_id=dev(z, 1 - c, me), device_id_type=MESH)
     for d in HOPS:
         @pl.when(valid(d))
         def _():
             pl.semaphore_signal(barrier, inc=1, device_id=dev(z + d, c, me), device_id_type=MESH)
-    each_piece(lambda p: local_copy(p).start())
-    whole_in.start()
-    pl.semaphore_wait(barrier, n + jnp.minimum(z, 1) + jnp.minimum(nz - 1 - z, 1))
+    local_copy(0).start()
+    pl.semaphore_wait(barrier, (3 if two else n) + jnp.minimum(z, 1) + jnp.minimum(nz - 1 - z, 1))
 
     def first_sends(p):
         issue_own(p, True)
@@ -168,8 +169,17 @@
         if p == 1:
             issue_own(p, False, to_end)
 
-    each_piece(lambda p: local_copy(p).wait())
-    each_piece(first_sends)
+    def rest(body):
+        for p in range(1, tail):
+            body(p)
+        each_tail(body)
+
+    local_copy(0).wait()
+    first_sends(0)
+    rest(lambda p: local_copy(p).start())
+    whole_in.start()
+    rest(lambda p: local_copy(p).wait())
+    rest(first_sends)
     whole_in.wait()
 
     @pl.when(jnp.logical_not(end))
@@ -203,12 +213,7 @@
 
         def rank_out(s, k):
             mine = rank.at[l, seg_rows(me), lanes(s)]
-            return copy_to(mine, mine, ag_s, ag_r, dev(z, c, other(k)))
-
-        sums = sbuf.at[pl.ds(0, (n - 1) * seg)]
-        ranks = rank.at[l, pl.ds(0, (n - 1) * seg)]
-        sums_all = copy_to(sums, sums, rs_s, ag_r, dev(z, 1 - c, me))
-        ranks_all = copy_to(ranks, ranks, ag_s, ag_r, dev(z, 1 - c, me))
+            return copy_to(mine, mine, ag_s, all_r, dev(z, c, other(k)))
 
         def reduce(s):
             acc = pf[seg_rows(me), lanes(s)]
@@ -219,6 +224,58 @@
             for k in range(1, n):
                 rank_out(s, k).start()
 
+        def mp_refs(kind, s):
+            at, here = lanes(s), rbuf.at[l, min(kind, 5), :, lanes(s)]
+            if kind < 4:
+                rows_at = half(peers[(2, 2, 0, 1)[kind]], (0, 1, 0, 1)[kind])
+                return sbuf.at[rows_at, at], here, rs_s, (rs_r if kind < 2 else cb_r).at[s]
+            if kind < 6:
+                return cbuf.at[kind - 4, :, at], here, cb_s, cb_r.at[s]
+            mine = (seg_rows(me), seg_rows(me), half(peers[0], 0), half(peers[1], 1))[kind - 6]
+            ref = rank.at[l, mine, at]
+            return ref, ref, ag_s, ag_r.at[s] if kind < 8 else all_r
+
+        def mp_out(kind, s):
+            src, dst, send, recv = mp_refs(kind, s)
+            return copy_to(src, dst, send, recv, dev(z, c, peers[TO_Y[kind]]))
+
+        def got(ref, sem):
+            copy_to(ref, ref, rs_s, sem, dev(z, 1 - c, me)).wait_recv()
+
+        def gone(ref, sem):
+            copy_to(ref, ref, sem, all_r, dev(z, 1 - c, me)).wait_send()
+
+        def sum_on(s):
+            at = lanes(s)
+            got(rbuf.at[l, pl.ds(0, 2), :, at], rs_r.at[s])
+            for h in range(2):
+                cbuf[h, :, at] = (pf[half(peers[1 - h], h), at]
+                                  + rbuf[l, h, :, at].astype(jnp.float32)).astype(jnp.bfloat16)
+                mp_out(4 + h, s).start()
+
+        def sum_up(s):
+            at = lanes(s)
+            got(rbuf.at[l, pl.ds(2, 4), :, at], cb_r.at[s])
+            for h in range(2):
+                acc = pf[half(me, h), at] + rbuf[l, 2 + h, :, at].astype(jnp.float32)
+                acc = acc + rbuf[l, 4 + h, :, at].astype(jnp.float32)
+                rank[l, half(me, h), at] = acc.astype(jnp.bfloat16)
+            for kind in (6, 7):
+                mp_out(kind, s).start()
+
+        def pass_on(s):
+            got(rank.at[l, pl.ds(0, 2 * seg), lanes(s)], ag_r.at[s])
+            for kind in (8, 9):
+                mp_out(kind, s).start()
+
+        def exchange(i, stages):
+            for lag, stage in stages:
+                @pl.when((i >= lag) & (i < nz + lag))
+                def _():
+                    stage(order(i - lag))
+
+        steps = ((1, sum_on), (2, sum_up), (3, pass_on)) if two else ((1, reduce),)
+
         last = l == layers - 1
         each_up = each_tail if last else lambda body: body(pu)
 
@@ -226,9 +283,12 @@
         def _(i):
             s = order(i)
 
-            @pl.when(i == nz - 1)
-            def _():
-                reduce(order(i - 1))
+            if two:
+                exchange(i, steps)
+            else:
+                @pl.when(i == nz - 1)
+                def _():
+                    reduce(order(i - 1))
 
             @pl.when(end & (i >= early(pv)))
             def _():
@@ -246,19 +306,28 @@
                                        preferred_element_type=jnp.float32)
             pf[:, lanes(s)] = part
             sbuf[:, lanes(s)] = part.astype(jnp.bfloat16)
-            for k in range(1, n):
-                sum_out(s, k).start()
-
-            @pl.when((i > 0) & (i < nz - 1))
-            def _():
-                reduce(order(i - 1))
+            if two:
+                for kind in range(4):
+                    mp_out(kind, s).start()
+            else:
+                for k in range(1, n):
+                    sum_out(s, k).start()
+
+                @pl.when((i > 0) & (i < nz - 1))
+                def _():
+                    reduce(order(i - 1))
 
         if pu + 2 < tail:
             issue_own(pu + 2, False)
         elif not last and layers > 2:
             issue_own(pv + 2, False)
 
-        reduce(order(nz - 1))
+        if two:
+            @pl.loop(nz, nz + 3)
+            def _(i):
+                exchange(i, steps)
+        else:
+            reduce(order(nz - 1))
 
         @pl.loop(0, nz - 1)
         def _(i):
@@ -297,9 +366,15 @@
                 for i in range(early(pv + 2)):
                     take(pv + 2, order(i))
 
-        ranks_all.wait_recv()
-        sums_all.wait_send()
-        ranks_all.wait_send()
+        if two:
+            got(rank.at[l, pl.ds(0, seg)], all_r)
+            gone(sbuf.at[pl.ds(0, 2 * seg)], rs_s)
+            gone(cbuf, cb_s)
+            gone(rank.at[l, pl.ds(0, 3 * seg)], ag_s)
+        else:
+            got(rank.at[l, pl.ds(0, (n - 1) * seg)], all_r)
+            gone(sbuf.at[pl.ds(0, (n - 1) * seg)], rs_s)
+            gone(rank.at[l, pl.ds(0, (n - 1) * seg)], ag_s)
 
         if last:
             @pl.when(end)
@@ -366,11 +441,13 @@
                 pltpu.VMEM((rows, cols), jnp.bfloat16),
                 pltpu.VMEM((rows, r), jnp.float32),
                 pltpu.VMEM((rows, r), jnp.bfloat16),
-                pltpu.VMEM((layers, n, rows // n, r), jnp.bfloat16),
+                pltpu.VMEM((layers, 6, rows // (2 * n), r) if n == 4 else (layers, n, rows // n, r),
+                           jnp.bfloat16),
                 pltpu.VMEM((layers, rows, r), jnp.bfloat16),
-                dma, dma((2 * layers,)), dma((pieces, nz)), dma((2 * layers,)), dma((2 * layers,)),
+                dma((2,)), dma((2 * layers,)), dma((pieces, nz)), dma((2 * layers,)), dma((2 * layers,)),
                 dma((layers, nz)), dma((layers - 1 + nb,)),
-                dma, dma((nz,)), dma, dma, dma,
+                pltpu.VMEM((2, rows // (2 * n), r), jnp.bfloat16),
+                dma, dma, dma, dma((nz,)), dma((nz,)), dma((nz,)), dma, dma,
             ],
             compiler_params=pltpu.CompilerParams(
                 collective_id=0, has_side_effects=True, vmem_limit_bytes=59*2**20),

time: 214 us -> 213 us (level)
  no operation moved by 1% of the time
where the time goes in v4:
time: 213 us
  Pallas kernels  211 us (99%)
    pallas_call x1, Pallas kernels, local(): pl.pallas_call(functools.partial(kernel, nz, n, native, nb), out_shape=pl...  211 us

profile of v4, /device:TPU:0, one launch (start us, length us, event | category | flops | bytes accessed | tf_op | source)
XLA Modules:
  0.0 212.9 jit_solution(13834615242479392410)
XLA Ops:
  0.0 210.9 %cross_layers.1 = bf16[1024,2048]{1,0:T(8,128)(2,1)S(1)} custom-call(bf16[3,2048,128]{2,1,0:T(8,128)(2,1)} %v_ref.1, bf16[3,128,2048]{2,1,0:T(8,128)(2,1)} %u_ref.1, bf16[1024,2048]{1,0:T(8,128)(2,1)} %x_ref.1, f32[3,2048]{1,0:T(4,128)} %b_ref.1), custom_call_target="tpu_custom_call" | custom-call | tf_op jit(solution)/shard_map/cross_layers/pallas_call | solution.py:433
  210.9 2.0 copy.6

commit v5 on v4

--- a/solution.py
+++ b/solution.py
@@ -12,7 +12,7 @@
 TO_Y = (0, 1, 0, 1, 1, 0, 0, 1, 1, 0)
 
 
-def kernel(nz, n, native, nb, v_ref, u_ref, x_ref, b_ref, out_ref, wv, wu, f_ref, pf, sbuf, rbuf,
+def kernel(nz, n, native, nb, v_ref, u_ref, x_ref, b_ref, out_ref, rank_ref, last_ref, kept_ref, wv, wu, f_ref, pf, sbuf, rbuf,
            rank, loc, zsend, zrecv, fsend, psend, vrecv, urecv, cbuf, rs_s, cb_s, ag_s, rs_r, cb_r, ag_r, all_r, in_s):
     layers, rs, cols = u_ref.shape
     rows = x_ref.shape[0]
@@ -23,15 +23,21 @@
     bw = cols // nb
 
     def at_sem(p):
+        if p is final:
+            return tail + nb - 1
         return tail + p[0] if isinstance(p, tuple) else p
 
     def factor(p):
         return tail if isinstance(p, tuple) else p
 
+    final = (None,)
+
     def each_tail(body):
-        @pl.loop(0, nb)
+        @pl.loop(0, nb - 1)
         def _(b):
             body((b,))
+
+        body(final)
 
     cb = 256 if cols % 256 == 0 else cols
     dp, me = lax.axis_index("dp"), lax.axis_index("mp")
@@ -56,6 +62,8 @@
         return (z + d >= 0) & (z + d < nz)
 
     def blk(p, s, cc):
+        if p is final:
+            return last_ref.at[pl.ds(pl.multiple_of((s * 2 + cc) * rs, rs), rs)]
         if isinstance(p, tuple):
             return wu.at[layers - 1, pl.ds(pl.multiple_of((s * 2 + cc) * rs, rs), rs),
                          pl.ds(pl.multiple_of(p[0] * bw, bw), bw)]
@@ -65,7 +73,9 @@
         return w.at[p // 2, pl.ds(pl.multiple_of((s * 2 + cc) * rs, rs), rs)]
 
     def local_copy(p):
-        if isinstance(p, tuple):
+        if p is final:
+            src = u_ref.at[layers - 1, :, pl.ds(cols - bw, bw)]
+        elif isinstance(p, tuple):
             src = u_ref.at[layers - 1, :, pl.ds(pl.multiple_of(p[0] * bw, bw), bw)]
         else:
             src = (v_ref if p % 2 == 0 else u_ref).at[p // 2]
@@ -88,13 +98,15 @@
 
     def landed(p, s):
         if isinstance(p, tuple):
-            return urecv.at[layers - 1 + p[0]]
+            return urecv.at[layers - 1 + (nb - 1 if p is final else p[0])]
         return urecv.at[p // 2] if p % 2 else vrecv.at[p // 2, s]
 
     def push(p, s):
         return copy_to(blk(p, s, c), blk(p, s, c), psend.at[factor(p)], landed(p, s), dev(z, 1 - c, me))
 
     def halves(p, count):
+        if p is final:
+            return last_ref.at[pl.ds(0, count * rs)]
         if isinstance(p, tuple):
             return wu.at[layers - 1, pl.ds(0, count * rs),
                          pl.ds(pl.multiple_of(p[0] * bw, bw), bw)]
@@ -181,6 +193,7 @@
     rest(lambda p: local_copy(p).wait())
     rest(first_sends)
     whole_in.wait()
+    kept_ref[...] = f_ref[:, pl.ds(cols - bw, bw)]
 
     @pl.when(jnp.logical_not(end))
     def _():
@@ -201,6 +214,8 @@
     for l in range(layers):
         pv, pu = 2 * l, 2 * l + 1
         cur = f_ref if l == 0 else out_ref
+        last = l == layers - 1
+        rk = rank_ref if last else rank.at[l]
 
         def sum_out(s, k):
             t = other(k)
@@ -212,7 +227,7 @@
             return copy_to(ref, ref, rs_s, rs_r.at[s], dev(z, 1 - c, me))
 
         def rank_out(s, k):
-            mine = rank.at[l, seg_rows(me), lanes(s)]
+            mine = rk.at[seg_rows(me), lanes(s)]
             return copy_to(mine, mine, ag_s, all_r, dev(z, c, other(k)))
 
         def reduce(s):
@@ -220,7 +235,7 @@
             sums_in(s).wait_recv()
             for k in range(1, n):
                 acc = acc + rbuf[l, other(k), :, lanes(s)].astype(jnp.float32)
-            rank[l, seg_rows(me), lanes(s)] = acc.astype(jnp.bfloat16)
+            rk[seg_rows(me), lanes(s)] = acc.astype(jnp.bfloat16)
             for k in range(1, n):
                 rank_out(s, k).start()
 
@@ -232,7 +247,7 @@
             if kind < 6:
                 return cbuf.at[kind - 4, :, at], here, cb_s, cb_r.at[s]
             mine = (seg_rows(me), seg_rows(me), half(peers[0], 0), half(peers[1], 1))[kind - 6]
-            ref = rank.at[l, mine, at]
+            ref = rk.at[mine, at]
             return ref, ref, ag_s, ag_r.at[s] if kind < 8 else all_r
 
         def mp_out(kind, s):
@@ -259,12 +274,12 @@
             for h in range(2):
                 acc = pf[half(me, h), at] + rbuf[l, 2 + h, :, at].astype(jnp.float32)
                 acc = acc + rbuf[l, 4 + h, :, at].astype(jnp.float32)
-                rank[l, half(me, h), at] = acc.astype(jnp.bfloat16)
+                rk[half(me, h), at] = acc.astype(jnp.bfloat16)
             for kind in (6, 7):
                 mp_out(kind, s).start()
 
         def pass_on(s):
-            got(rank.at[l, pl.ds(0, 2 * seg), lanes(s)], ag_r.at[s])
+            got(rk.at[pl.ds(0, 2 * seg), lanes(s)], ag_r.at[s])
             for kind in (8, 9):
                 mp_out(kind, s).start()
 
@@ -276,7 +291,6 @@
 
         steps = ((1, sum_on), (2, sum_up), (3, pass_on)) if two else ((1, reduce),)
 
-        last = l == layers - 1
         each_up = each_tail if last else lambda body: body(pu)
 
         @pl.loop(0, nz)
@@ -367,37 +381,44 @@
                     take(pv + 2, order(i))
 
         if two:
-            got(rank.at[l, pl.ds(0, seg)], all_r)
+            got(rk.at[pl.ds(0, seg)], all_r)
             gone(sbuf.at[pl.ds(0, 2 * seg)], rs_s)
             gone(cbuf, cb_s)
-            gone(rank.at[l, pl.ds(0, 3 * seg)], ag_s)
+            gone(rk.at[pl.ds(0, 3 * seg)], ag_s)
         else:
-            got(rank.at[l, pl.ds(0, (n - 1) * seg)], all_r)
+            got(rk.at[pl.ds(0, (n - 1) * seg)], all_r)
             gone(sbuf.at[pl.ds(0, (n - 1) * seg)], rs_s)
-            gone(rank.at[l, pl.ds(0, (n - 1) * seg)], ag_s)
+            gone(rk.at[pl.ds(0, (n - 1) * seg)], ag_s)
 
         if last:
             @pl.when(end)
             def _():
-                take((0,), order(nz - 1))
+                take((0,) if nb > 1 else final, order(nz - 1))
 
         def finish(p):
             @pl.when(end)
             def _():
                 if last:
-                    @pl.when(p[0] < nb - 1)
-                    def _():
-                        take((p[0] + 1,), order(nz - 1))
+                    if p is not final:
+                        @pl.when(p[0] < nb - 2)
+                        def _():
+                            take((p[0] + 1,), order(nz - 1))
+
+                        @pl.when(p[0] == nb - 2)
+                        def _():
+                            take(final, order(nz - 1))
                 else:
                     take(p, order(nz - 1))
 
             pushed(p).wait_recv()
+            if p is final:
+                return
             width, base = (bw, p[0] * bw) if last else (cols, 0)
 
             @pl.loop(0, width // cb)
             def _(j):
                 at = pl.ds(pl.multiple_of(base + j * cb, cb), cb)
-                cross = jnp.dot(rank[l], wu[l, :, at], preferred_element_type=jnp.float32)
+                cross = jnp.dot(rk[...], wu[l, :, at], preferred_element_type=jnp.float32)
                 cross = cross + b_ref[l, at][None, :]
                 out_ref[:, at] = (f_ref[:, at].astype(jnp.float32) * cross
                                   + cur[:, at].astype(jnp.float32)).astype(jnp.bfloat16)
@@ -415,6 +436,23 @@
                 sent(psend, p, nz)
 
 
+def last_block(x_ref, rank_ref, u_ref, b_ref, f_ref, y_ref, block, sems):
+    cols, bw = x_ref.shape[1], u_ref.shape[1]
+    done, at = pl.ds(0, cols - bw), pl.ds(cols - bw, bw)
+    store = pltpu.make_async_copy(block, y_ref.at[:, at], sems.at[0])
+    if cols > bw:
+        ready = pltpu.make_async_copy(x_ref.at[:, done], y_ref.at[:, done], sems.at[1])
+        ready.start()
+    cross = jnp.dot(rank_ref[...], u_ref[...], preferred_element_type=jnp.float32)
+    cross = cross + b_ref[b_ref.shape[0] - 1, at][None, :]
+    block[...] = (f_ref[...].astype(jnp.float32) * cross
+                  + x_ref[:, at].astype(jnp.float32)).astype(jnp.bfloat16)
+    store.start()
+    if cols > bw:
+        ready.wait()
+    store.wait()
+
+
 def solution(mesh):
     n = mesh.shape["mp"]
     nz = mesh.shape["dp"] // 2
@@ -423,18 +461,20 @@
         layers, rs, cols = u_weight.shape
         rows = features.shape[0]
         r = rs * nz * 2
-        nb = 8 if cols % 2048 == 0 else 1
+        nb = cols // 256 if cols % 256 == 0 else 1
         pieces = 2 * layers - 1 + nb
         native = rs % 128 == 0
         v = v_weight if native else jnp.swapaxes(v_weight, 1, 2)
         vm = pl.BlockSpec(memory_space=pltpu.VMEM)
         hbm = pl.BlockSpec(memory_space=pl.ANY)
         dma = pltpu.SemaphoreType.DMA
-        return pl.pallas_call(
+        crossed, rank, u_last, kept = pl.pallas_call(
             functools.partial(kernel, nz, n, native, nb),
-            out_shape=pltpu.VMEM((rows, cols), jnp.bfloat16),
+            out_shape=(pltpu.VMEM((rows, cols), jnp.bfloat16), pltpu.VMEM((rows, r), jnp.bfloat16),
+                       pltpu.VMEM((r, cols // nb), jnp.bfloat16),
+                       pltpu.VMEM((rows, cols // nb), jnp.bfloat16)),
             in_specs=[hbm, hbm, hbm, vm],
-            out_specs=vm,
+            out_specs=(vm, vm, vm, vm),
             scratch_shapes=[
                 pltpu.VMEM((layers, nz, cols, 2 * rs) if native else (layers, r, cols), jnp.bfloat16),
                 pltpu.VMEM((layers, r, cols), jnp.bfloat16),
@@ -443,16 +483,25 @@
                 pltpu.VMEM((rows, r), jnp.bfloat16),
                 pltpu.VMEM((layers, 6, rows // (2 * n), r) if n == 4 else (layers, n, rows // n, r),
                            jnp.bfloat16),
-                pltpu.VMEM((layers, rows, r), jnp.bfloat16),
+                pltpu.VMEM((max(layers - 1, 1), rows, r), jnp.bfloat16),
                 dma((2,)), dma((2 * layers,)), dma((pieces, nz)), dma((2 * layers,)), dma((2 * layers,)),
                 dma((layers, nz)), dma((layers - 1 + nb,)),
                 pltpu.VMEM((2, rows // (2 * n), r), jnp.bfloat16),
                 dma, dma, dma, dma((nz,)), dma((nz,)), dma((nz,)), dma, dma,
             ],
             compiler_params=pltpu.CompilerParams(
-                collective_id=0, has_side_effects=True, vmem_limit_bytes=59*2**20),
+                collective_id=0, has_side_effects=True, vmem_limit_bytes=55 * 2**20),
             name="cross_layers",
         )(v, u_weight, features, cross_bias)
+        return pl.pallas_call(
+            last_block,
+            out_shape=jax.ShapeDtypeStruct((rows, cols), jnp.bfloat16),
+            in_specs=[vm, vm, vm, vm, vm],
+            out_specs=hbm,
+            scratch_shapes=[pltpu.VMEM((rows, cols // nb), jnp.bfloat16), dma((2,))],
+            compiler_params=pltpu.CompilerParams(vmem_limit_bytes=16 * 2**20),
+            name="last_block",
+        )(crossed, rank, u_last, cross_bias, kept)
 
     return jax.shard_map(
         local,

time: 213 us -> 212 us (level)
    pallas_call x1 -> x2, Pallas kernels: 211 us -> 212 us  [the longest x1 210 us: local(): pl.pallas_call(functools.partial(kernel, nz, n, native, nb), out_shape=(p...]
where the time goes in v5:
time: 212 us
  Pallas kernels  212 us (100%)
    pallas_call x1, Pallas kernels, local(): pl.pallas_call(functools.partial(kernel, nz, n, native, nb), out_shape=(p...  210 us

profile of v5, /device:TPU:0, one launch (start us, length us, event | category | flops | bytes accessed | tf_op | source)
XLA Modules:
  0.0 212.2 jit_solution(15972259572347033338)
XLA Ops:
  0.0 0.0 copy-start
  0.0 210.2 %cross_layers.1 = (bf16[1024,2048]{1,0:T(8,128)(2,1)S(1)}, bf16[1024,1024]{1,0:T(8,128)(2,1)S(1)}, bf16[1024,256]{1,0:T(8,128)(2,1)S(1)}, bf16[1024,256]{1,0:T(8,128)(2,1)S(1)}) custom-call(bf16[3,2048,128]{2,1,0:T(8,128)(2,1)} %v_ref.1, bf16[3,128,2048]{2,1,0:T(8,128)(2,1)} %u_ref.1, bf16[1024,2048]{1,0:T(8,128)(2,1)} %x_ref.1, f32[3,2048]{1,0:T(4,128)} %b_ref.3), custom_call_target="tpu_custom_call" | custom-call | tf_op jit(solution)/shard_map/cross_layers/pallas_call | solution.py:471
  210.2 0.0 copy-done
  210.2 2.0 last_block.1
Async XLA Ops:
  0.0 210.2 %copy-start = (f32[3,2048]{1,0:T(4,128)S(1)}, f32[3,2048]{1,0:T(4,128)}, u32[]{:S(2)}) copy-start(f32[3,2048]{1,0:T(4,128)} %b_ref.3) | copy-start | bytes 73732

commit v6 on v5

--- a/solution.py
+++ b/solution.py
@@ -83,17 +83,20 @@
 
     def direct(p, k):
         return copy_to(blk(p, z, c), blk(p, z, c), zsend.at[factor(p)],
-                       zrecv.at[at_sem(p), z], dev(z + HOPS[k], c, me))
+                       zrecv.at[at_sem(p), z + min(HOPS[k], 0)], dev(z + HOPS[k], c, me))
+
+    def slot(s):
+        return jnp.where(s > z, s - 1, s)
 
     def arrival(p, s):
         return copy_to(blk(p, s, c), blk(p, s, c), fsend.at[factor(p)],
-                       zrecv.at[at_sem(p), s], dev(z, 1 - c, me))
+                       zrecv.at[at_sem(p), slot(s)], dev(z, 1 - c, me))
 
     def relays(s):
         return ((s > z) & (z >= 1)) | ((s < z) & (z <= nz - 2))
 
     def relay(p, s):
-        return copy_to(blk(p, s, c), blk(p, s, c), fsend.at[factor(p)], zrecv.at[at_sem(p), s],
+        return copy_to(blk(p, s, c), blk(p, s, c), fsend.at[factor(p)], zrecv.at[at_sem(p), slot(s)],
                        dev(jnp.where(s > z, z - 1, z + 1), c, me))
 
     def landed(p, s):
@@ -193,7 +196,6 @@
     rest(lambda p: local_copy(p).wait())
     rest(first_sends)
     whole_in.wait()
-    kept_ref[...] = f_ref[:, pl.ds(cols - bw, bw)]
 
     @pl.when(jnp.logical_not(end))
     def _():
@@ -207,6 +209,8 @@
         issue_own(2, False)
     else:
         each_tail(lambda p: issue_own(p, False))
+
+    kept_ref[...] = f_ref[:, pl.ds(cols - bw, bw)]
 
     def early(p):
         return {0: 0, 2: min(2, nz)}.get(p, 1)
@@ -484,7 +488,7 @@
                 pltpu.VMEM((layers, 6, rows // (2 * n), r) if n == 4 else (layers, n, rows // n, r),
                            jnp.bfloat16),
                 pltpu.VMEM((max(layers - 1, 1), rows, r), jnp.bfloat16),
-                dma((2,)), dma((2 * layers,)), dma((pieces, nz)), dma((2 * layers,)), dma((2 * layers,)),
+                dma((2,)), dma((2 * layers,)), dma((pieces, nz - 1)), dma((2 * layers,)), dma((2 * layers,)),
                 dma((layers, nz)), dma((layers - 1 + nb,)),
                 pltpu.VMEM((2, rows // (2 * n), r), jnp.bfloat16),
                 dma, dma, dma, dma((nz,)), dma((nz,)), dma((nz,)), dma, dma,

time: 212 us -> 212 us (level)
  no operation moved by 1% of the time
where the time goes in v6:
time: 212 us
  Pallas kernels  212 us (100%)
    pallas_call x1, Pallas kernels, local(): pl.pallas_call(functools.partial(kernel, nz, n, native, nb), out_shape=(p...  210 us

profile of v6, /device:TPU:0, one launch (start us, length us, event | category | flops | bytes accessed | tf_op | source)
XLA Modules:
  0.0 212.1 jit_solution(3354072281854798511)
XLA Ops:
  0.0 0.0 copy-start
  0.0 210.1 %cross_layers.1 = (bf16[1024,2048]{1,0:T(8,128)(2,1)S(1)}, bf16[1024,1024]{1,0:T(8,128)(2,1)S(1)}, bf16[1024,256]{1,0:T(8,128)(2,1)S(1)}, bf16[1024,256]{1,0:T(8,128)(2,1)S(1)}) custom-call(bf16[3,2048,128]{2,1,0:T(8,128)(2,1)} %v_ref.1, bf16[3,128,2048]{2,1,0:T(8,128)(2,1)} %u_ref.1, bf16[1024,2048]{1,0:T(8,128)(2,1)} %x_ref.1, f32[3,2048]{1,0:T(4,128)} %b_ref.3), custom_call_target="tpu_custom_call" | custom-call | tf_op jit(solution)/shard_map/cross_layers/pallas_call | solution.py:475
  210.1 0.0 copy-done
  210.1 2.0 last_block.1
Async XLA Ops:
  0.0 210.1 %copy-start = (f32[3,2048]{1,0:T(4,128)S(1)}, f32[3,2048]{1,0:T(4,128)}, u32[]{:S(2)}) copy-start(f32[3,2048]{1,0:T(4,128)} %b_ref.3) | copy-start | bytes 73732
